TPU v7x, 32 devices: a whole 2x2x4 slice. The times are simulated.
32 devices in a mesh: seq: 8 (over z, y), head: 4 (over x, core).
Axes of the slice: x: 2, y: 2, z: 4, core: 2. Of those that a mesh axis runs over, the one named last changes fastest.
Arguments:
- hidden_states: bfloat16 [2048, 1536], P('seq', 'head'), may hold values from -60 to 60
- feature_q: bfloat16 [1536, 384], P(None, 'head'), may hold values from -0.15625 to 0.15625
- feature_k: bfloat16 [1536, 384], P(None, 'head'), may hold values from -0.15625 to 0.15625
- value_w: bfloat16 [1536, 1536], P(None, 'head'), may hold values from -0.15625 to 0.15625
- window_q: bfloat16 [1536, 1536], P(None, 'head'), may hold values from -0.15625 to 0.15625
- window_k: bfloat16 [1536, 1536], P(None, 'head'), may hold values from -0.15625 to 0.15625
- norm_gain: float32 [1536], P('head'), may hold values from 0.5 to 1.5
Outputs:
- mixed: bfloat16 [2048, 1536], P('seq', 'head')
All inputs are finite; a program needn't handle non-finite values.
Results may differ from a plain program's by a relative error of at most 0.007.
Values may be sent and summed in bfloat16 or wider, within the bound.
A program may use at most 128 MiB of HBM per device.

v0:
```python
import jax
import jax.numpy as jnp
import numpy as np
from jax import lax
from jax.sharding import PartitionSpec as P

FK = 16
HV = 64
WINDOW_HEAD_SIZE = 64
WIN = 64
HIGH_ACCURACY = lax.Precision.HIGHEST


def from_behind(shard, axis, by):
    devices = lax.axis_size(axis)
    pairs = [(i, i + by) for i in range(devices) if 0 <= i + by < devices]
    return lax.ppermute(shard, axis, pairs)


def prefix_2(value, axis, join, neutral):
    count, mine = (lax.axis_size(axis), lax.axis_index(axis))
    pieces = lax.all_gather(value, axis)
    so_far = jnp.full_like(value, 0) + jnp.asarray(neutral, value.dtype)

    def lap(position, so_far):
        longer = join(so_far, pieces[position])
        return jnp.where(position < mine, longer, so_far)

    return lax.fori_loop(0, count - 1, lap, so_far)


def expand(x):
    lead = x.shape[:-1]
    width = x.shape[-1]
    ones = jnp.ones(lead + (1,), jnp.float32)
    upper, lower = np.triu_indices(width)
    weight = np.where(upper == lower, 0.5**0.5, 1.0).astype(np.float32)
    quad = x[..., upper] * x[..., lower] * weight
    return jnp.concatenate([ones, x, quad], axis=-1)


def add_states(earlier, later):
    return earlier + later


def body(hidden_states, feature_q, feature_k, value_w, window_q, window_k, norm_gain):
    rows = hidden_states.shape[0]
    heads = feature_q.shape[1] // FK
    offset = lax.axis_index("seq") * rows
    whole = lax.all_gather(hidden_states, "head", axis=1, tiled=True)
    query = (jnp.dot(whole, feature_q, preferred_element_type=jnp.float32) * FK ** (-0.25)).reshape(
        rows, heads, FK
    )
    key = (jnp.dot(whole, feature_k, preferred_element_type=jnp.float32) * FK ** (-0.25)).reshape(
        rows, heads, FK
    )
    wquery = jnp.dot(whole, window_q, preferred_element_type=jnp.float32).astype(jnp.bfloat16)
    wkey = jnp.dot(whole, window_k, preferred_element_type=jnp.float32).astype(jnp.bfloat16)
    values_ext = jnp.dot(whole, value_w, preferred_element_type=jnp.float32).astype(jnp.bfloat16)
    prev_keys, prev_values = from_behind((wkey[rows - WIN :], values_ext[rows - WIN :]), "seq", 1)
    key_rows_full = jnp.concatenate([prev_keys, wkey], axis=0)
    values_all = jnp.concatenate([prev_values, values_ext], axis=0)
    value3 = values_ext.reshape(rows, heads, HV)
    phi_q = expand(query)
    phi_k = expand(key)
    width = phi_k.shape[-1]
    local_state = jnp.einsum(
        "lhf,lhv->fhv", phi_k, value3.astype(jnp.float32), precision=HIGH_ACCURACY
    ).reshape(width, heads * HV)
    prefix = prefix_2(local_state, "seq", add_states, jnp.zeros_like(local_state))
    inner = jnp.einsum("lhf,mhf->hlm", query, key, precision=HIGH_ACCURACY)
    kernel = 1.0 + inner + 0.5 * inner * inner
    index_rows = jnp.arange(rows, dtype=jnp.int32)
    causal = index_rows[:, None] >= index_rows[None, :]
    kernel = jnp.where(causal[None], kernel, 0.0).astype(jnp.bfloat16)
    intra = jnp.einsum("hlm,mhv->lhv", kernel, value3, preferred_element_type=jnp.float32)
    cross = jnp.einsum(
        "lhf,fhv->lhv", phi_q, prefix.reshape(width, heads, HV), precision=HIGH_ACCURACY
    )
    linear = intra + cross
    scale = lax.rsqrt(jnp.mean(linear * linear, axis=-1, keepdims=True) + 1e-05)
    normed = linear * scale * norm_gain.reshape(heads, HV)
    query_weight3 = wquery.reshape(rows, heads, WINDOW_HEAD_SIZE)
    key_tensor3 = key_rows_full.reshape(rows + WIN, heads, WINDOW_HEAD_SIZE)
    window_logits = jnp.einsum(
        "qxo,bxo->xqb", query_weight3, key_tensor3, preferred_element_type=jnp.float32
    ) * WINDOW_HEAD_SIZE ** (-0.5)
    query_pos = offset + index_rows[:, None]
    key_pos = offset - WIN + jnp.arange(rows + WIN, dtype=jnp.int32)[None, :]
    valid = (key_pos <= query_pos) & (key_pos > query_pos - WIN) & (key_pos >= 0)
    window_logits = jnp.where(valid[None], window_logits, -1e30)
    top = jnp.max(window_logits, axis=-1, keepdims=True)
    expw = jnp.exp(window_logits - top)
    weights = (expw / jnp.sum(expw, axis=-1, keepdims=True)).astype(jnp.bfloat16)
    window = jnp.einsum(
        "hlm,mhv->lhv",
        weights,
        values_all.reshape(rows + WIN, heads, HV),
        preferred_element_type=jnp.float32,
    )
    return (normed + window).astype(jnp.bfloat16).reshape(rows, heads * HV)


def solution(mesh):
    in_specs = (
        P("seq", "head"),
        P(None, "head"),
        P(None, "head"),
        P(None, "head"),
        P(None, "head"),
        P(None, "head"),
        P("head"),
    )
    out_specs = P("seq", "head")
    return jax.shard_map(body, mesh=mesh, in_specs=in_specs, out_specs=out_specs, check_vma=False)
```

profile of v0, /device:TPU:0, one launch (start us, length us, event | category | flops | bytes accessed | tf_op | source)
XLA Modules:
  0.0 101.9 jit_solution(2306110077940659043)
XLA Ops:
  6.5 10.4 %all_gather.6 = bf16[256,1536]{1,0:T(8,128)(2,1)S(1)} all-gather(bf16[256,384]{1,0:T(8,128)(2,1)} %param.19), channel_id=1, replica_groups=mesh['seq'=8,'head'=4] {'head'}, dimensions={1}, use_global_device_ids=true | all-gather | bytes 983040 | tf_op jit(solution)/shard_map/all_gather | solution.py:50
  17.0 1.5 %convolution_multiply_fusion = f32[256,96]{0,1:T(8,128)S(1)} fusion(bf16[256,1536]{1,0:T(8,128)(2,1)S(1)} %all_gather.6, bf16[1536,96]{0,1:T(8,128)(2,1)} %param.21), kind=kOutput, calls=%fused_computation.22 | convolution fusion | flops 75522048 | bytes 1179648 | tf_op jit(solution)/shard_map/dot_general | solution.py:54
  18.5 0.0 copy-start.9
  18.5 0.1 copy.42
  18.6 0.5 copy-done.9
  19.1 0.8 gather_fusion
  19.9 0.8 gather_fusion.1
  20.7 1.6 %convolution_multiply_fusion.1 = f32[256,96]{0,1:T(8,128)S(1)} fusion(bf16[256,1536]{1,0:T(8,128)(2,1)} %copy-done.1, bf16[1536,96]{0,1:T(8,128)(2,1)} %param.20), kind=kOutput, calls=%fused_computation.23 | convolution fusion | flops 75522048 | bytes 1179648 | tf_op jit(solution)/shard_map/dot_general | solution.py:51
  22.3 0.6 copy-done.7
  22.9 0.1 copy.48
  23.0 1.8 %gather_fusion.2 = f32[136,256,6]{1,2,0:T(8,128)} fusion(f32[256,6,16]{0,1,2:T(8,128)S(1)} %copy.48, s32[1024]{0:T(1024)S(1)} %pad_clamp_fusion.1), kind=kCustom, calls=%fused_computation.2 | custom fusion | bytes 1671712 | tf_op jit(solution)/shard_map/gather | solution.py:38
  24.8 1.8 %gather_fusion.3 = f32[136,256,6]{1,2,0:T(8,128)} fusion(f32[256,6,16]{0,1,2:T(8,128)S(1)} %copy.48, s32[1024]{0:T(1024)S(1)} %pad_clamp_fusion), kind=kCustom, calls=%fused_computation.3 | custom fusion | bytes 1671712 | tf_op jit(solution)/shard_map/gather | solution.py:38
  26.6 2.4 %convolution_convert_fusion.2 = bf16[256,384]{1,0:T(8,128)(2,1)} fusion(bf16[256,1536]{1,0:T(8,128)(2,1)} %copy-done.1, bf16[1536,384]{1,0:T(8,128)(2,1)S(1)} %copy-done), kind=kOutput, calls=%fused_computation.20 | convolution fusion | flops 302088192 | bytes 2162688 | tf_op jit(solution)/shard_map/dot_general | solution.py:59
  29.0 1.8 %copy.41 = bf16[256,384]{0,1:T(8,128)(2,1)} copy(bf16[256,384]{1,0:T(8,128)(2,1)} %convolution_convert_fusion.2) | data formatting | bytes 393216 | tf_op jit(solution)/shard_map/convert_element_type | solution.py:59
  30.8 3.5 %fusion.21 = (f32[256,6,136]{0,2,1:T(8,128)}, f32[256,6,136]{0,2,1:T(8,128)S(1)}) fusion(f32[136,256,6]{1,2,0:T(8,128)} %gather_fusion.3, f32[136,256,6]{1,2,0:T(8,128)} %gather_fusion.2, f32[136]{0:T(256)S(1)} %copy-done.14, f32[136,256,6]{1,2,0:T(8,128)S(1)} %gather_fusion.1, f32[136,256,6]{1,2,0:T(8,128)S(1)} %gather_fusion), kind=kLoop, calls=%fused_computation.38 | loop fusion | flops 835584 | bytes 5014048 | tf_op jit(solution)/shard_map/mul | solution.py:38
  34.2 0.8 fusion.8
  35.1 0.8 copy.46
  35.9 0.0 all-gather.2.cloned.1.call-update
  35.9 1.8 %convolution_convert_fusion = bf16[256,384]{1,0:T(8,128)(2,1)S(1)} fusion(bf16[256,1536]{1,0:T(8,128)(2,1)S(1)} %copy-done.2, bf16[1536,384]{1,0:T(8,128)(2,1)} %param.24), kind=kOutput, calls=%fused_computation.18 | convolution fusion | flops 302088192 | bytes 2162688 | tf_op jit(solution)/shard_map/dot_general | solution.py:58
  37.8 3.6 %collective-permute-start.1 = (bf16[64,384]{1,0:T(8,128)(2,1)S(1)}, bf16[64,384]{1,0:T(8,128)(2,1)S(1)}, u32[]{:S(2)}, u32[]{:S(2)}) collective-permute-start(bf16[64,384]{1,0:T(8,128)(2,1)S(1)} %slice.17), channel_id=1, source_target_pairs={{0,4},{4,8},{8,12},{12,16},{16,20},{20,24},{24,28},{1,5},{5,9},{9,... | collective-permute-start | bytes 147464 | tf_op jit(solution)/shard_map/ppermute | solution.py:17
  41.4 4.0 %collective-permute-start = (bf16[64,384]{1,0:T(8,128)(2,1)S(1)}, bf16[64,384]{1,0:T(8,128)(2,1)}, u32[]{:S(2)}, u32[]{:S(2)}) collective-permute-start(bf16[64,384]{1,0:T(8,128)(2,1)S(1)} %slice.16), channel_id=1, source_target_pairs={{0,4},{4,8},{8,12},{12,16},{16,20},{20,24},{24,28},{1,5},{5,9},{9,... | collective-permute-start | bytes 147464 | tf_op jit(solution)/shard_map/ppermute | solution.py:17
  45.5 0.0 copy-start.17
  45.5 1.7 %fusion.4 = bf16[6,256,256]{2,1,0:T(8,128)(2,1)S(1)} fusion(f32[256,6,16]{0,2,1:T(8,128)S(1)} %bitcast.52, f32[256,6,16]{0,2,1:T(8,128)S(1)} %bitcast.56, pred[256,256]{1,0:T(8,128)(4,1)S(1)} %iota_compare_fusion), kind=kOutput, calls=%fused_computation.13 | convolution fusion | flops 77856768 | bytes 1048576 | tf_op jit(solution)/shard_map/lhf,mhf->hlm/dot_general | solution.py:71
  47.2 0.4 fusion.33
  47.6 0.0 copy-start.13
  47.6 0.6 convolution_convert_fusion.1
  48.2 0.2 and_and_fusion
  48.3 0.1 copy.53
  48.5 0.1 mul.81
  48.6 0.0 collective-permute-done.1
  48.6 0.2 copy.54
  48.8 0.8 pad_maximum_fusion
  49.7 0.2 copy.52
  49.9 2.1 %fusion.32 = (f32[6,256]{1,0:T(8,128)S(1)}, f32[6,256,320]{1,2,0:T(8,128)}) fusion(pred[256,320]{0,1:T(8,128)(4,1)S(1)} %and_and_fusion, bf16[256,6,64]{0,2,1:T(8,128)(2,1)S(1)} %bitcast.59, bf16[320,6,64]{0,2,1:T(8,128)(2,1)S(1)} %bitcast.58), kind=kOutput, calls=%fused_computation.61 | convolution fusion | flops 64880960 | bytes 2496512 | tf_op jit(solution)/shard_map/sub | solution.py:93
  51.9 32.9 %all-gather.2.cloned.1.call-done = f32[8,153,384]{2,1,0:T(8,128)} async-done(((f32[1,153,384]{2,1,0:T(8,128)}), f32[8,153,384]{2,1,0:T(8,128)}) %all-gather.2.cloned.1.call-update) | async-done | bytes 1880080 | tf_op jit(solution)/shard_map/all_gather | solution.py:22
  84.8 7.3 %while.14 = (s32[]{:T(128)}, f32[153,384]{1,0:T(8,128)S(1)}, s32[]{:T(128)}, f32[8,153,384]{2,1,0:T(8,128)}, s32[]{:T(128)}, /*index=5*/s32[]{:T(128)}) while((s32[]{:T(128)}, f32[153,384]{1,0:T(8,128)S(1)}, s32[]{:T(128)}, f32[8,153,384]{2,1,0:T(8,128)}, s32[]{:T(128)}, /*index=5*/s32[]{:T(128)}) %tuple.36), condition=%wide.region_1.2_spmd.clone, body=%wide.region_0.1_spmd.clone.sunk | while | flops 176260 | bytes 705117 | solution.py:29
  84.8 1.1 %add_select_fusion.2 = f32[153,384]{1,0:T(8,128)S(1)} fusion(f32[153,384]{1,0:T(8,128)S(1)} %get-tuple-element.148, f32[8,153,384]{2,1,0:T(8,128)} %get-tuple-element.156, s32[]{:T(128)} %get-tuple-element.147, pred[]{:T(512)S(6)} %compare.3, pred[]{:T(512)S(6)} %lt.21), kind=kLoop, calls=%fused_computation.4.clone.1 | loop fusion | flops 176256 | bytes 705030 | tf_op jit(solution)/shard_map/while/body/eval_jaxpr/jit(_where)/select_n | solution.py:27
  85.9 1.0 add_select_fusion.2
  87.0 1.0 add_select_fusion.2
  88.0 1.0 add_select_fusion.2
  89.1 1.0 add_select_fusion.2
  90.1 1.0 add_select_fusion.2
  91.1 1.0 add_select_fusion.2
  92.2 0.2 copy.47
  92.4 0.8 multiply_reduce_fusion
  93.2 0.6 copy-done.18
  93.9 0.3 fusion.7
  94.2 0.8 copy.55
  (46 shorter events, 0.2 us)
Async XLA Ops:
  6.5 20.0 %copy-start = (bf16[1536,384]{1,0:T(8,128)(2,1)S(1)}, bf16[1536,384]{1,0:T(8,128)(2,1)}, u32[]{:S(2)}) copy-start(bf16[1536,384]{1,0:T(8,128)(2,1)} %param.22) | copy-start | bytes 3538948
  6.5 12.0 %copy-start.15 = (s32[136]{0:T(256)S(1)}, s32[136]{0:T(256)}, u32[]{:S(2)}) copy-start(s32[136]{0:T(256)} %constant.74) | copy-start | bytes 1636
  6.5 12.6 %copy-start.16 = (s32[136]{0:T(256)S(1)}, s32[136]{0:T(256)}, u32[]{:S(2)}) copy-start(s32[136]{0:T(256)} %constant.75) | copy-start | bytes 1636
  6.5 78.3 %all-gather.2.cloned.1.call-start = ((), (), s32[]{:S(2)}) async-start(), calls=%async_computation | async-start | bytes 2211840 | tf_op jit(solution)/shard_map/all_gather | solution.py:22
  17.0 1.6 %copy-start.1 = (bf16[256,1536]{1,0:T(8,128)(2,1)}, bf16[256,1536]{1,0:T(8,128)(2,1)S(1)}, u32[]{:S(2)}) copy-start(bf16[256,1536]{1,0:T(8,128)(2,1)S(1)} %all_gather.6) | copy-start | bytes 2359300
  18.5 0.6 copy-start.9
  22.3 0.6 copy-start.7
  26.6 4.2 %copy-start.14 = (f32[136]{0:T(256)S(1)}, f32[136]{0:T(256)}, u32[]{:S(2)}) copy-start(f32[136]{0:T(256)} %constant.71.clone) | copy-start | bytes 1636
  30.7 3.5 %copy-start.11 = (f32[153]{0:T(256)}, f32[153]{0:T(256)S(1)}, u32[]{:S(2)}) copy-start(f32[153]{0:T(256)S(1)} %pad.7.clone) | copy-start | bytes 1840
  30.7 3.5 %copy-start.4 = (bf16[256,384]{0,1:T(8,128)(2,1)S(1)}, bf16[256,384]{0,1:T(8,128)(2,1)}, u32[]{:S(2)}) copy-start(bf16[256,384]{0,1:T(8,128)(2,1)} %copy.41) | copy-start | bytes 589828
  30.7 3.5 %copy-start.10 = (f32[256,96]{0,1:T(8,128)S(1)}, f32[256,96]{0,1:T(8,128)}, u32[]{:S(2)}) copy-start(f32[256,96]{0,1:T(8,128)} %copy-done.9) | copy-start | bytes 294916
  34.2 1.7 %copy-start.2 = (bf16[256,1536]{1,0:T(8,128)(2,1)S(1)}, bf16[256,1536]{1,0:T(8,128)(2,1)}, u32[]{:S(2)}) copy-start(bf16[256,1536]{1,0:T(8,128)(2,1)} %copy-done.1) | copy-start | bytes 2359300
  35.0 6.3 %copy-start.6 = (bf16[256,384]{1,0:T(8,128)(2,1)S(1)}, bf16[256,384]{1,0:T(8,128)(2,1)}, u32[]{:S(2)}) copy-start(bf16[256,384]{1,0:T(8,128)(2,1)} %convolution_convert_fusion.2) | copy-start | bytes 589828
  35.1 10.4 %copy-start.8 = (f32[256,96]{0,1:T(8,128)S(1)}, f32[256,96]{0,1:T(8,128)}, u32[]{:S(2)}) copy-start(f32[256,96]{0,1:T(8,128)} %copy-done.7) | copy-start | bytes 294916
  37.8 9.4 %copy-start.5 = (bf16[256,384]{0,1:T(8,128)(2,1)S(1)}, bf16[256,384]{0,1:T(8,128)(2,1)}, u32[]{:S(2)}) copy-start(bf16[256,384]{0,1:T(8,128)(2,1)} %copy.41) | copy-start | bytes 589828
  37.8 10.7 %collective-permute-start.1 = (bf16[64,384]{1,0:T(8,128)(2,1)S(1)}, bf16[64,384]{1,0:T(8,128)(2,1)S(1)}, u32[]{:S(2)}, u32[]{:S(2)}) collective-permute-start(bf16[64,384]{1,0:T(8,128)(2,1)S(1)} %slice.17), channel_id=1, source_target_pairs={{0,4},{4,8},{8,12},{12,16},{16,20},{20,24},{24,28},{1,5},{5,9},{9,... | collective-permute-start | bytes 147464 | tf_op jit(solution)/shard_map/ppermute | solution.py:17
  41.4 7.4 %collective-permute-start = (bf16[64,384]{1,0:T(8,128)(2,1)S(1)}, bf16[64,384]{1,0:T(8,128)(2,1)}, u32[]{:S(2)}, u32[]{:S(2)}) collective-permute-start(bf16[64,384]{1,0:T(8,128)(2,1)S(1)} %slice.16), channel_id=1, source_target_pairs={{0,4},{4,8},{8,12},{12,16},{16,20},{20,24},{24,28},{1,5},{5,9},{9,... | collective-permute-start | bytes 147464 | tf_op jit(solution)/shard_map/ppermute | solution.py:17
  45.5 2.1 %copy-start.17 = (bf16[1536,384]{1,0:T(8,128)(2,1)S(1)}, bf16[1536,384]{1,0:T(8,128)(2,1)}, u32[]{:S(2)}) copy-start(bf16[1536,384]{1,0:T(8,128)(2,1)} %param.23) | copy-start | bytes 3538948
  47.6 0.9 copy-start.13
  84.8 7.5 %copy-start.3 = (f32[256,6,136]{0,2,1:T(8,128)S(1)}, f32[256,6,136]{0,2,1:T(8,128)}, u32[]{:S(2)}) copy-start(f32[256,6,136]{0,2,1:T(8,128)} %get-tuple-element.108) | copy-start | bytes 2506756
  84.8 7.5 %copy-start.12 = (f32[153]{0:T(256)S(1)}, f32[153]{0:T(256)}, u32[]{:S(2)}) copy-start(f32[153]{0:T(256)} %copy-done.11) | copy-start | bytes 1840
  92.3 1.5 %copy-start.18 = (f32[6,256,320]{1,2,0:T(8,128)S(1)}, f32[6,256,320]{1,2,0:T(8,128)}, u32[]{:S(2)}) copy-start(f32[6,256,320]{1,2,0:T(8,128)} %get-tuple-element.111) | copy-start | bytes 5898244
Sparse Core Ops, SparseCore 0:
  36.1 48.7 all-gather.1
where the time goes:
time: 102 us
  waiting for transfers between devices  32.9 us (32%)
  matrix products  14 us (14%)
  between operations  13.8 us (14%)
  other arithmetic  11.7 us (11%)
  local copies, waits for them, and re-layouts  11.4 us (11%)
  blocking collectives  10.4 us (10%)
  starting transfers between devices  7.6 us (7%)
    all_gather x1, waiting for transfers between devices, prefix_2(): pieces = lax.all_gather(value, axis)  32.9 us
    all_gather x1, blocking collectives, body(): whole = lax.all_gather(hidden_states, 'head', axis=1, tiled=True)  10.4 us
    ppermute x2, starting transfers between devices, from_behind(): return lax.ppermute(shard, axis, pairs)  7.6 us
    select_n x7, other arithmetic, lap(): return jnp.where(position < mine, longer, so_far)  7.18 us
    gather x4, local copies, waits for them, and re-layouts, expand(): quad = x[..., upper] * x[..., lower] * weight  5.12 us
    mul x1, other arithmetic, expand(): quad = x[..., upper] * x[..., lower] * weight  3.47 us
    dot_general x1, matrix products, body(): jnp.dot(whole, value_w, preferred_element_type=jnp.float32)  2.4 us
    sub x1, matrix products, body(): expw = jnp.exp(window_logits - top)  2.07 us
  transfers between devices with their start and end apart: 3, of which 1 were waited for; matrix products, arithmetic and copies ran while one was open for 8% of the time, Pallas kernels for 0%

commit v1 on v0

--- a/solution.py
+++ b/solution.py
@@ -47,7 +47,7 @@
     rows = hidden_states.shape[0]
     heads = feature_q.shape[1] // FK
     offset = lax.axis_index("seq") * rows
-    whole = lax.all_gather(hidden_states, "head", axis=1, tiled=True)
+    whole = jnp.concatenate(lax.all_gather(hidden_states, "head"), axis=1)
     query = (jnp.dot(whole, feature_q, preferred_element_type=jnp.float32) * FK ** (-0.25)).reshape(
         rows, heads, FK
     )

time: 102 us -> 98.4 us (0.965)
  matrix products: 14 us -> 9.71 us
  other arithmetic: 11.7 us -> 12.8 us
    dot_general x1, matrix products: 2.4 us -> 0.6 us  [body(): jnp.dot(whole, value_w, preferred_element_type=jnp.float32)]
    convert_element_type x1, local copies, waits for them, and re-layouts: 1.75 us -> 0.15 us  [body(): jnp.dot(whole, value_w, preferred_element_type=jnp.float32)]
    dot_general x1, matrix products: 1.57 us -> 0.27 us  [body(): jnp.dot(whole, feature_q, preferred_element_type=jnp.float32)]
    dot_general x1, matrix products: 1.52 us -> 0.27 us  [body(): jnp.dot(whole, feature_k, preferred_element_type=jnp.float32)]
  transfers between devices with their start and end apart: 3 -> 3, of which waited for: 1 -> 1; matrix products, arithmetic and copies ran while one was open for 8% -> 10% of each run, Pallas kernels for 0% -> 0%
where the time goes in v1:
time: 98.4 us; the launch traced here: 97.8 us
  waiting for transfers between devices  31.9 us (32%)
  between operations  13.7 us (14%)
  other arithmetic  12.8 us (13%)
  local copies, waits for them, and re-layouts  11.7 us (12%)
  blocking collectives  10.4 us (11%)
  matrix products  9.71 us (10%)
  starting transfers between devices  7.46 us (8%)
    all_gather x1, waiting for transfers between devices, prefix_2(): pieces = lax.all_gather(value, axis)  31.9 us
    all_gather x1, blocking collectives, body(): whole = jnp.concatenate(lax.all_gather(hidden_states, 'head'), axis=1)  10.4 us
    ppermute x2, starting transfers between devices, from_behind(): return lax.ppermute(shard, axis, pairs)  7.46 us
    select_n x7, other arithmetic, lap(): return jnp.where(position < mine, longer, so_far)  7.19 us
    gather x4, local copies, waits for them, and re-layouts, expand(): quad = x[..., upper] * x[..., lower] * weight  6.14 us
    mul x1, other arithmetic, expand(): quad = x[..., upper] * x[..., lower] * weight  3.79 us
    sub x1, matrix products, body(): expw = jnp.exp(window_logits - top)  2.07 us
  transfers between devices with their start and end apart: 3, of which 1 were waited for; matrix products, arithmetic and copies ran while one was open for 10% of the time, Pallas kernels for 0%

profile of v1, /device:TPU:0, one launch (start us, length us, event | category | flops | bytes accessed | tf_op | source)
XLA Modules:
  0.0 97.8 jit_solution(8925416471909589476)
XLA Ops:
  6.5 10.4 %all-gather = bf16[1024,384]{1,0:T(8,128)(2,1)S(1)} all-gather(bf16[256,384]{1,0:T(8,128)(2,1)} %param.19), channel_id=2, replica_groups=mesh['seq'=8,'head'=4] {'head'}, dimensions={0}, use_global_device_ids=true | all-gather | bytes 983040 | tf_op jit(solution)/shard_map/all_gather | solution.py:50
  16.9 0.3 copy.57
  17.2 0.3 convolution_multiply_fusion
  17.5 0.1 copy.59
  17.6 0.0 copy-done.13
  17.6 0.5 copy-done.6
  18.2 0.8 gather_fusion
  19.0 1.8 %gather_fusion.1 = f32[136,256,6]{1,2,0:T(8,128)} fusion(f32[256,6,16]{0,1,2:T(8,128)S(1)} %copy.59, s32[1024]{0:T(1024)S(1)} %pad_clamp_fusion), kind=kCustom, calls=%fused_computation.1 | custom fusion | bytes 1671712 | tf_op jit(solution)/shard_map/gather | solution.py:38
  20.7 0.3 convolution_multiply_fusion.1
  21.0 0.6 copy-done.3
  21.7 0.1 copy.65
  21.7 1.8 %gather_fusion.2 = f32[136,256,6]{1,2,0:T(8,128)} fusion(f32[256,6,16]{0,1,2:T(8,128)S(1)} %copy.65, s32[1024]{0:T(1024)S(1)} %pad_clamp_fusion.1), kind=kCustom, calls=%fused_computation.2 | custom fusion | bytes 1671712 | tf_op jit(solution)/shard_map/gather | solution.py:38
  23.5 1.8 %gather_fusion.3 = f32[136,256,6]{1,2,0:T(8,128)} fusion(f32[256,6,16]{0,1,2:T(8,128)S(1)} %copy.65, s32[1024]{0:T(1024)S(1)} %pad_clamp_fusion), kind=kCustom, calls=%fused_computation.3 | custom fusion | bytes 1671712 | tf_op jit(solution)/shard_map/gather | solution.py:38
  25.3 0.6 convolution_convert_fusion.2
  25.9 0.1 copy.58
  26.1 3.8 %fusion.21 = (f32[256,6,136]{0,2,1:T(8,128)}, f32[256,6,136]{0,2,1:T(8,128)S(1)}) fusion(f32[136,256,6]{1,2,0:T(8,128)} %gather_fusion.3, f32[136,256,6]{1,2,0:T(8,128)} %gather_fusion.2, f32[136]{0:T(256)S(1)} %copy-done.12, f32[136,256,6]{1,2,0:T(8,128)} %gather_fusion.1, f32[136,256,6]{1,2,0:T(8,128)S(1)} %gather_fusion), kind=kLoop, calls=%fused_computation.38 | loop fusion | flops 835584 | bytes 5014048 | tf_op jit(solution)/shard_map/mul | solution.py:38
  29.9 0.8 fusion.8
  30.7 0.9 copy.63
  31.6 0.0 all-gather.3.cloned.1.call-update
  31.6 1.9 %convolution_convert_fusion = bf16[256,384]{1,0:T(8,128)(2,1)S(1)} fusion(bf16[256,1536]{0,1:T(8,128)(2,1)S(1)} %bitcast.54, bf16[1536,384]{1,0:T(8,128)(2,1)} %param.24), kind=kOutput, calls=%fused_computation.18 | convolution fusion | flops 302088192 | bytes 2162688 | tf_op jit(solution)/shard_map/dot_general | solution.py:58
  33.5 0.6 slice.17
  34.1 4.0 %collective-permute-start.1 = (bf16[64,384]{1,0:T(8,128)(2,1)}, bf16[64,384]{1,0:T(8,128)(2,1)}, u32[]{:S(2)}, u32[]{:S(2)}) collective-permute-start(bf16[64,384]{1,0:T(8,128)(2,1)} %slice.17), channel_id=1, source_target_pairs={{0,4},{4,8},{8,12},{12,16},{16,20},{20,24},{24,28},{1,5},{5,9},{9,... | collective-permute-start | bytes 147464 | tf_op jit(solution)/shard_map/ppermute | solution.py:17
  38.1 3.4 %collective-permute-start = (bf16[64,384]{1,0:T(8,128)(2,1)S(1)}, bf16[64,384]{1,0:T(8,128)(2,1)}, u32[]{:S(2)}, u32[]{:S(2)}) collective-permute-start(bf16[64,384]{1,0:T(8,128)(2,1)S(1)} %slice.16), channel_id=1, source_target_pairs={{0,4},{4,8},{8,12},{12,16},{16,20},{20,24},{24,28},{1,5},{5,9},{9,... | collective-permute-start | bytes 147464 | tf_op jit(solution)/shard_map/ppermute | solution.py:17
  41.6 1.7 %fusion.4 = bf16[6,256,256]{2,1,0:T(8,128)(2,1)S(1)} fusion(f32[256,6,16]{0,2,1:T(8,128)S(1)} %bitcast.62, f32[256,6,16]{0,2,1:T(8,128)S(1)} %bitcast.66, pred[256,256]{1,0:T(8,128)(4,1)S(1)} %iota_compare_fusion), kind=kOutput, calls=%fused_computation.13 | convolution fusion | flops 77856768 | bytes 1048576 | tf_op jit(solution)/shard_map/lhf,mhf->hlm/dot_general | solution.py:71
  43.3 0.4 fusion.33
  43.7 0.6 convolution_convert_fusion.1
  44.3 0.2 and_and_fusion
  44.5 0.1 copy.70
  44.6 0.1 mul.81
  44.7 0.8 pad_maximum_fusion.1
  45.5 0.2 copy.71
  45.8 0.8 pad_maximum_fusion
  46.6 0.2 copy.69
  46.8 2.1 %fusion.32 = (f32[6,256]{1,0:T(8,128)S(1)}, f32[6,256,320]{1,2,0:T(8,128)}) fusion(pred[256,320]{0,1:T(8,128)(4,1)S(1)} %and_and_fusion, bf16[256,6,64]{0,2,1:T(8,128)(2,1)S(1)} %bitcast.69, bf16[320,6,64]{0,2,1:T(8,128)(2,1)S(1)} %bitcast.68), kind=kOutput, calls=%fused_computation.61 | convolution fusion | flops 64880960 | bytes 2496512 | tf_op jit(solution)/shard_map/sub | solution.py:93
  48.9 31.9 %all-gather.3.cloned.1.call-done = f32[8,153,384]{2,1,0:T(8,128)} async-done(((f32[1,153,384]{2,1,0:T(8,128)}), f32[8,153,384]{2,1,0:T(8,128)}) %all-gather.3.cloned.1.call-update) | async-done | bytes 1880080 | tf_op jit(solution)/shard_map/all_gather | solution.py:22
  80.8 7.3 %while.14 = (s32[]{:T(128)}, f32[153,384]{1,0:T(8,128)S(1)}, s32[]{:T(128)}, f32[8,153,384]{2,1,0:T(8,128)}, s32[]{:T(128)}, /*index=5*/s32[]{:T(128)}) while((s32[]{:T(128)}, f32[153,384]{1,0:T(8,128)S(1)}, s32[]{:T(128)}, f32[8,153,384]{2,1,0:T(8,128)}, s32[]{:T(128)}, /*index=5*/s32[]{:T(128)}) %tuple.36), condition=%wide.region_1.2_spmd.clone, body=%wide.region_0.1_spmd.clone.sunk | while | flops 176260 | bytes 705117 | solution.py:29
  80.8 1.1 %add_select_fusion.2 = f32[153,384]{1,0:T(8,128)S(1)} fusion(f32[153,384]{1,0:T(8,128)S(1)} %get-tuple-element.148, f32[8,153,384]{2,1,0:T(8,128)} %get-tuple-element.156, s32[]{:T(128)} %get-tuple-element.147, pred[]{:T(512)S(6)} %compare.3, pred[]{:T(512)S(6)} %lt.21), kind=kLoop, calls=%fused_computation.4.clone.1 | loop fusion | flops 176256 | bytes 705030 | tf_op jit(solution)/shard_map/while/body/eval_jaxpr/jit(_where)/select_n | solution.py:27
  81.9 1.0 %add_select_fusion.2 = f32[153,384]{1,0:T(8,128)S(1)} fusion(f32[153,384]{1,0:T(8,128)S(1)} %get-tuple-element.148, f32[8,153,384]{2,1,0:T(8,128)} %get-tuple-element.156, s32[]{:T(128)} %get-tuple-element.147, pred[]{:T(512)S(6)} %compare.3, pred[]{:T(512)S(6)} %lt.21), kind=kLoop, calls=%fused_computation.4.clone.1 | loop fusion | flops 176256 | bytes 705030 | tf_op jit(solution)/shard_map/while/body/eval_jaxpr/jit(_where)/select_n | solution.py:27
  82.9 1.0 %add_select_fusion.2 = f32[153,384]{1,0:T(8,128)S(1)} fusion(f32[153,384]{1,0:T(8,128)S(1)} %get-tuple-element.148, f32[8,153,384]{2,1,0:T(8,128)} %get-tuple-element.156, s32[]{:T(128)} %get-tuple-element.147, pred[]{:T(512)S(6)} %compare.3, pred[]{:T(512)S(6)} %lt.21), kind=kLoop, calls=%fused_computation.4.clone.1 | loop fusion | flops 176256 | bytes 705030 | tf_op jit(solution)/shard_map/while/body/eval_jaxpr/jit(_where)/select_n | solution.py:27
  84.0 1.0 %add_select_fusion.2 = f32[153,384]{1,0:T(8,128)S(1)} fusion(f32[153,384]{1,0:T(8,128)S(1)} %get-tuple-element.148, f32[8,153,384]{2,1,0:T(8,128)} %get-tuple-element.156, s32[]{:T(128)} %get-tuple-element.147, pred[]{:T(512)S(6)} %compare.3, pred[]{:T(512)S(6)} %lt.21), kind=kLoop, calls=%fused_computation.4.clone.1 | loop fusion | flops 176256 | bytes 705030 | tf_op jit(solution)/shard_map/while/body/eval_jaxpr/jit(_where)/select_n | solution.py:27
  85.0 1.0 %add_select_fusion.2 = f32[153,384]{1,0:T(8,128)S(1)} fusion(f32[153,384]{1,0:T(8,128)S(1)} %get-tuple-element.148, f32[8,153,384]{2,1,0:T(8,128)} %get-tuple-element.156, s32[]{:T(128)} %get-tuple-element.147, pred[]{:T(512)S(6)} %compare.3, pred[]{:T(512)S(6)} %lt.21), kind=kLoop, calls=%fused_computation.4.clone.1 | loop fusion | flops 176256 | bytes 705030 | tf_op jit(solution)/shard_map/while/body/eval_jaxpr/jit(_where)/select_n | solution.py:27
  86.0 1.0 %add_select_fusion.2 = f32[153,384]{1,0:T(8,128)S(1)} fusion(f32[153,384]{1,0:T(8,128)S(1)} %get-tuple-element.148, f32[8,153,384]{2,1,0:T(8,128)} %get-tuple-element.156, s32[]{:T(128)} %get-tuple-element.147, pred[]{:T(512)S(6)} %compare.3, pred[]{:T(512)S(6)} %lt.21), kind=kLoop, calls=%fused_computation.4.clone.1 | loop fusion | flops 176256 | bytes 705030 | tf_op jit(solution)/shard_map/while/body/eval_jaxpr/jit(_where)/select_n | solution.py:27
  87.1 1.0 %add_select_fusion.2 = f32[153,384]{1,0:T(8,128)S(1)} fusion(f32[153,384]{1,0:T(8,128)S(1)} %get-tuple-element.148, f32[8,153,384]{2,1,0:T(8,128)} %get-tuple-element.156, s32[]{:T(128)} %get-tuple-element.147, pred[]{:T(512)S(6)} %compare.3, pred[]{:T(512)S(6)} %lt.21), kind=kLoop, calls=%fused_computation.4.clone.1 | loop fusion | flops 176256 | bytes 705030 | tf_op jit(solution)/shard_map/while/body/eval_jaxpr/jit(_where)/select_n | solution.py:27
  88.1 0.2 copy.64
  88.3 0.9 multiply_reduce_fusion
  89.2 0.6 copy-done.15
  89.8 0.3 fusion.7
  90.2 0.8 copy.72
  (41 shorter events, 0.1 us)
Async XLA Ops:
  6.5 18.8 %copy-start = (bf16[1536,384]{1,0:T(8,128)(2,1)S(1)}, bf16[1536,384]{1,0:T(8,128)(2,1)}, u32[]{:S(2)}) copy-start(bf16[1536,384]{1,0:T(8,128)(2,1)} %param.22) | copy-start | bytes 3538948
  6.5 10.7 %copy-start.9 = (bf16[1536,96]{0,1:T(8,128)(2,1)S(1)}, bf16[1536,96]{0,1:T(8,128)(2,1)}, u32[]{:S(2)}) copy-start(bf16[1536,96]{0,1:T(8,128)(2,1)} %param.21) | copy-start | bytes 884740
  6.5 74.2 %all-gather.3.cloned.1.call-start = ((), (), s32[]{:S(2)}) async-start(), calls=%async_computation | async-start | bytes 2211840 | tf_op jit(solution)/shard_map/all_gather | solution.py:22
  16.9 0.7 copy-start.13
  16.9 1.2 %copy-start.14 = (s32[136]{0:T(256)S(1)}, s32[136]{0:T(256)}, u32[]{:S(2)}) copy-start(s32[136]{0:T(256)} %constant.75) | copy-start | bytes 1636
  17.5 0.6 copy-start.6
  18.9 1.8 %copy-start.10 = (bf16[1536,96]{0,1:T(8,128)(2,1)S(1)}, bf16[1536,96]{0,1:T(8,128)(2,1)}, u32[]{:S(2)}) copy-start(bf16[1536,96]{0,1:T(8,128)(2,1)} %param.20) | copy-start | bytes 884740
  21.0 0.6 copy-start.3
  25.3 0.8 copy-start.12
  26.1 3.8 %copy-start.7 = (f32[256,96]{0,1:T(8,128)S(1)}, f32[256,96]{0,1:T(8,128)}, u32[]{:S(2)}) copy-start(f32[256,96]{0,1:T(8,128)} %copy-done.6) | copy-start | bytes 294916
  30.7 10.9 %copy-start.4 = (f32[256,96]{0,1:T(8,128)S(1)}, f32[256,96]{0,1:T(8,128)}, u32[]{:S(2)}) copy-start(f32[256,96]{0,1:T(8,128)} %copy-done.3) | copy-start | bytes 294916
  30.7 10.9 %copy-start.8 = (f32[256,96]{0,1:T(8,128)S(1)}, f32[256,96]{0,1:T(8,128)}, u32[]{:S(2)}) copy-start(f32[256,96]{0,1:T(8,128)} %copy-done.6) | copy-start | bytes 294916
  34.1 10.6 %collective-permute-start.1 = (bf16[64,384]{1,0:T(8,128)(2,1)}, bf16[64,384]{1,0:T(8,128)(2,1)}, u32[]{:S(2)}, u32[]{:S(2)}) collective-permute-start(bf16[64,384]{1,0:T(8,128)(2,1)} %slice.17), channel_id=1, source_target_pairs={{0,4},{4,8},{8,12},{12,16},{16,20},{20,24},{24,28},{1,5},{5,9},{9,... | collective-permute-start | bytes 147464 | tf_op jit(solution)/shard_map/ppermute | solution.py:17
  38.1 7.6 %collective-permute-start = (bf16[64,384]{1,0:T(8,128)(2,1)S(1)}, bf16[64,384]{1,0:T(8,128)(2,1)}, u32[]{:S(2)}, u32[]{:S(2)}) collective-permute-start(bf16[64,384]{1,0:T(8,128)(2,1)S(1)} %slice.16), channel_id=1, source_target_pairs={{0,4},{4,8},{8,12},{12,16},{16,20},{20,24},{24,28},{1,5},{5,9},{9,... | collective-permute-start | bytes 147464 | tf_op jit(solution)/shard_map/ppermute | solution.py:17
  41.6 2.0 %copy-start.2 = (bf16[1536,384]{1,0:T(8,128)(2,1)S(1)}, bf16[1536,384]{1,0:T(8,128)(2,1)}, u32[]{:S(2)}) copy-start(bf16[1536,384]{1,0:T(8,128)(2,1)} %param.23) | copy-start | bytes 3538948
  43.7 0.9 copy-start.11
  80.8 7.5 %copy-start.1 = (f32[256,6,136]{0,2,1:T(8,128)S(1)}, f32[256,6,136]{0,2,1:T(8,128)}, u32[]{:S(2)}) copy-start(f32[256,6,136]{0,2,1:T(8,128)} %get-tuple-element.108) | copy-start | bytes 2506756
  80.8 7.5 %copy-start.5 = (f32[256,96]{0,1:T(8,128)S(1)}, f32[256,96]{0,1:T(8,128)}, u32[]{:S(2)}) copy-start(f32[256,96]{0,1:T(8,128)} %copy-done.3) | copy-start | bytes 294916
  88.3 1.5 %copy-start.15 = (f32[6,256,320]{1,2,0:T(8,128)S(1)}, f32[6,256,320]{1,2,0:T(8,128)}, u32[]{:S(2)}) copy-start(f32[6,256,320]{1,2,0:T(8,128)} %get-tuple-element.111) | copy-start | bytes 5898244
Sparse Core Ops, SparseCore 0:
  31.7 49.0 all-gather.2
